TPU v7x, 256 devices: a whole 4x4x8 slice. The times are simulated.
256 devices in a mesh: gx: 8 (over x, y_lo), gy: 32 (over y_hi, z, core).
Axes of the slice: x: 4, y: 4 (y_hi: 2, y_lo: 2; y = y_hi * 2 + y_lo), z: 8, core: 2. Of those that a mesh axis runs over, the one named last changes fastest.
Arguments:
- density: float32 [256, 1024, 256], P('gx', 'gy'), may hold values from -6 to 6
- flux_east: float32 [256, 1024, 256], P('gx', 'gy'), may hold values from -6 to 6
- flux_north: float32 [256, 1024, 256], P('gx', 'gy'), may hold values from -6 to 6
- flux_up: float32 [256, 1024, 256], P('gx', 'gy'), may hold values from -6 to 6
- theta_pert: float32 [256, 1024, 256], P('gx', 'gy'), may hold values from -2 to 4
- sound_coef: bfloat16 [256, 1024, 256], P('gx', 'gy'), may hold values from 0.5 to 2
- vert_inverse: float32 [512, 512], replicated, may hold values from -1 to 1
Outputs:
- density_new: float32 [256, 1024, 256], P('gx', 'gy')
- east_new: float32 [256, 1024, 256], P('gx', 'gy')
- north_new: float32 [256, 1024, 256], P('gx', 'gy')
- upward_new: float32 [256, 1024, 256], P('gx', 'gy')
- theta_new: float32 [256, 1024, 256], P('gx', 'gy')
All inputs are finite; a program needn't handle non-finite values.
Results may differ from a plain program's by a relative error of at most 0.0003.
Values sent between devices are 32-bit elements; how exact they have to be, the bound alone decides.
A program may use at most 64 MiB of HBM per device.

v0:
```python
import jax
import jax.numpy as jnp
from jax import lax
from jax.experimental import pallas as pl
from jax.experimental.pallas import tpu as pltpu
from jax.sharding import PartitionSpec as P

SUBSTEPS = 6
courant = 0.45
damping = 0.1
MESH = pl.DeviceIdType.MESH
f32 = jnp.float32
bf16 = jnp.bfloat16

N = 32
LV = 256
LANES = 128
HALVES = (0, 1)
ROWS = N * N
STRIDE = 40
PADDED = (N + 4) * STRIDE + 8
BX = 4
BR = BX * N
BLOCKS = N // BX
RING = (("x", -1), ("x", N), ("y", -1), ("y", N))
FIRST = (("x", N - 1), ("x", 0), ("y", N - 1), ("y", 0))
SECOND = (("x", N - 2), ("x", 1), ("y", N - 2), ("y", 1))
OUTER = (("x", -2), ("x", N + 1), ("y", -2), ("y", N + 1))
CORNER_FROM = ((N - 1, N - 1), (N - 1, 0), (0, N - 1), (0, 0))
CORNER_AT = ((-1, -1), (-1, N), (N, -1), (N, N))


def lanes(half):
    return pl.ds(half * LANES, LANES)


def row(x, y):
    return (x + 2) * STRIDE + 8 + y


def line(side, dx=0, dy=0):
    axis, at = side
    if axis == "x":
        return pl.ds(row(at + dx, dy), N)
    return pl.ds(row(dx, at + dy), N, STRIDE)


def compact(side):
    axis, at = side
    if axis == "x":
        return pl.ds(at * N, N)
    return pl.ds(at, N, N)


def split(value):
    high = value.astype(bf16)
    return high, (value - high.astype(f32)).astype(bf16)


def kernel(
    rho_h, u_h, v_h, w_h, th_h, cf_h, m_h,
    rho_o, u_o, v_o, w_o, th_o,
    rho, us, vs, ws, th, cf, cc, h0, hh, ms, mh, ml, xh, xl, qs, ga, gb,
    bth, bxh, bxl, bh0, bh, bcc,
    cs, cr, ss, sr, gs, gr, ks, kr,
    lsem, csem, crem, ssem, srem, gsem, grem, ksem, krem,
):
    gx = lax.axis_index("gx")
    gy = lax.axis_index("gy")
    nx = lax.axis_size("gx")
    ny = lax.axis_size("gy")
    xm, xp = lax.rem(gx + nx - 1, nx), lax.rem(gx + 1, nx)
    ym, yp = lax.rem(gy + ny - 1, ny), lax.rem(gy + 1, ny)
    side_to = ((xp, gy), (xm, gy), (gx, yp), (gx, ym))
    corner_to = ((xp, yp), (xp, ym), (xm, yp), (xm, ym))

    loads = []

    def load(src, dst):
        copy = pltpu.make_async_copy(src, dst, lsem.at[len(loads)])
        copy.start()
        loads.append(copy)
        return copy

    load_th = [load(th_h.at[:, lanes(k)], th.at[k]) for k in HALVES]
    load_cf = load(cf_h, cf)
    load_u = [load(u_h.at[:, lanes(k)], us.at[k, pl.ds(0, ROWS)]) for k in HALVES]
    load_v = [load(v_h.at[:, :, lanes(k)], vs.at[k, :, pl.ds(0, N)]) for k in HALVES]
    load_w = [load(w_h.at[:, lanes(k)], ws.at[k]) for k in HALVES]
    load_m = load(m_h, ms)
    load_rho = [load(rho_h.at[:, lanes(k)], rho.at[k]) for k in HALVES]

    barrier = pltpu.get_barrier_semaphore()
    for to in side_to + corner_to:
        pl.semaphore_signal(barrier, inc=1, device_id=to, device_id_type=MESH)

    def grid_of(n):
        return ga if n % 2 == 1 else gb

    vflat = vs.reshape(2, N * STRIDE, LANES)
    for k in HALVES:
        us[k, pl.ds(ROWS, N), :] = jnp.zeros((N, LANES), f32)
        vs[k, :, pl.ds(N, STRIDE - N), :] = jnp.zeros((N, STRIDE - N, LANES), f32)
    ks[...] = jnp.zeros_like(ks)

    for copy in load_th:
        copy.wait()
    load_cf.wait()

    def first_g(b, carry):
        at = pl.ds(pl.multiple_of(b * BR, BR), BR)
        for k in HALVES:
            c = -courant * cf[at, lanes(k)].astype(f32)
            cc[k, at, :] = c
            g = c * th[k, at, :]
            for i in range(BX):
                ga[k, pl.ds(pl.multiple_of((b * BX + i + 2) * STRIDE + 8, 8), N), :] = g[i * N : (i + 1) * N]
        return carry

    lax.fori_loop(0, BLOCKS, first_g, 0)
    for copy in load_u + load_v:
        copy.wait()
    for k in HALVES:
        for s in range(4):
            cs[s, 0, k] = ga[k, line(FIRST[s]), :]
        cs[1, 1, k] = us[k, pl.ds(0, N), :]
        cs[3, 1, k] = vflat[k, pl.ds(0, N, STRIDE), :]
        for c in range(4):
            x, y = CORNER_FROM[c]
            ks[0, c, pl.ds(k, 1), :] = ga[k, pl.ds(row(x, y), 1), :]
            ks[0, c, pl.ds(2 + k, 1), :] = us[k, pl.ds(x * N + y, 1), :]
            ks[0, c, pl.ds(4 + k, 1), :] = vflat[k, pl.ds(x * STRIDE + y, 1), :]

    pl.semaphore_wait(barrier, 8)

    def send(src, dst, sent, got, to):
        return pltpu.make_async_remote_copy(
            src_ref=src, dst_ref=dst, send_sem=sent, recv_sem=got,
            device_id=to, device_id_type=MESH,
        )

    def critical(s):
        part = pl.ds(0, 1 + s % 2)
        return send(cs.at[s, part], cr.at[s, part], csem.at[s], crem.at[s], side_to[s])

    def second(s):
        return send(ss.at[s], sr.at[s], ssem.at[s], srem.at[s], side_to[s])

    def side(slot, s):
        return send(gs.at[slot, s], gr.at[slot, s], gsem.at[slot, s], grem.at[slot, s], side_to[s])

    def corner(slot, c):
        return send(ks.at[slot, c], kr.at[slot, c], ksem.at[slot, c], krem.at[slot, c], corner_to[c])

    for s in range(4):
        critical(s).start()
    for c in range(4):
        corner(0, c).start()

    def first_h(x, carry):
        at = pl.ds(pl.multiple_of(x * N, N), N)
        nxt = pl.ds(pl.multiple_of(x * N + N, N), N)
        for k in HALVES:
            h0[k, at, :] = (us[k, nxt, :] - us[k, at, :]) + (
                vs[k, x, pl.ds(1, N), :] - vs[k, x, pl.ds(0, N), :]
            )
        return carry

    lax.fori_loop(0, N, first_h, 0)
    for copy in load_w:
        copy.wait()
    for k in HALVES:
        for s in range(4):
            edge = compact(FIRST[s])
            ss[s, 0, k] = th[k, edge, :]
            ss[s, 1, k] = ws[k, edge, :]
            ss[s, 2, k] = cc[k, edge, :]
            ss[s, 3, k] = h0[k, edge, :]
            ss[s, 4, k] = ga[k, line(SECOND[s]), :]
    for s in range(4):
        second(s).start()

    def first_w(b, carry):
        at = pl.ds(pl.multiple_of(b * BR, BR), BR)
        for k in HALVES:
            high, low = split(ws[k, at, :])
            xh[at, lanes(k)] = high
            xl[at, lanes(k)] = low
        return carry

    lax.fori_loop(0, BLOCKS, first_w, 0)
    load_m.wait()
    for i in range(4):
        for j in range(4):
            high, low = split(ms[pl.ds(i * 128, 128), pl.ds(j * 128, 128)].T)
            mh[pl.ds(j * 128, 128), pl.ds(i * 128, 128)] = high
            ml[pl.ds(j * 128, 128), pl.ds(i * 128, 128)] = low

    def early_state(s, k):
        at = pl.ds(N * 4 + s * N, N)
        from_main = compact(SECOND[s])
        bth[k, at, :] = th[k, from_main, :]
        bcc[k, at, :] = cc[k, from_main, :]
        high, low = split(ws[k, from_main, :])
        bxh[at, lanes(k)] = high
        bxl[at, lanes(k)] = low

    for k in HALVES:
        for s in range(4):
            early_state(s, k)

    for copy in load_rho:
        copy.wait()
    for s in range(4):
        critical(s).wait_recv()
    for k in HALVES:
        for s in range(4):
            ga[k, line(RING[s]), :] = cr[s, 0, k]
        us[k, pl.ds(ROWS, N), :] = cr[1, 1, k]
        last_x = pl.ds(ROWS - N, N)
        h0[k, last_x, :] = h0[k, last_x, :] + cr[1, 1, k]
        last_y = pl.ds(N - 1, N, N)
        h0[k, last_y, :] = h0[k, last_y, :] + cr[3, 1, k]
        for s in range(4):
            bh0[k, pl.ds(N * 4 + s * N, N), :] = h0[k, compact(SECOND[s]), :]

    first_lane = lax.broadcasted_iota(jnp.int32, (BR, LV), 1) == 0

    def product(high, low):
        q = jnp.dot(high, mh[...], preferred_element_type=f32)
        q = q + jnp.dot(low, mh[...], preferred_element_type=f32)
        return q + jnp.dot(high, ml[...], preferred_element_type=f32)

    def vertical(upward):
        below = jnp.where(first_lane, 0.0, pltpu.roll(upward, 1, 1))
        return upward - below

    def laplacian(grid, k, edge):
        here = grid[k, line(edge), :]
        around = (grid[k, line(edge, -1), :] + grid[k, line(edge, 1), :]) + (
            grid[k, line(edge, 0, -1), :] + grid[k, line(edge, 0, 1), :]
        )
        return around - 4.0 * here, here

    def batch(n, edges, base):
        grid = grid_of(n)
        at = pl.ds(base, 4 * N)
        total = []
        for k in HALVES:
            laps, heres = zip(*[laplacian(grid, k, edge) for edge in edges])
            total.append(jnp.concatenate(heres, axis=0))
            h = bh0[k, at, :] + jnp.concatenate(laps, axis=0)
            bh[k, at, :] = h
            high, low = split(bth[k, at, :] - courant * h)
            bxh[at, pl.ds(LV + k * LANES, LANES)] = high
            bxl[at, pl.ds(LV + k * LANES, LANES)] = low
        q = product(bxh[at, :], bxl[at, :])
        diff = vertical(q[:, :LV])
        out = []
        for k in HALVES:
            part = slice(k * LANES, (k + 1) * LANES)
            high, low = split(q[:, part])
            bxh[at, lanes(k)] = high
            bxl[at, lanes(k)] = low
            theta = q[:, LV + k * LANES : LV + (k + 1) * LANES]
            bth[k, at, :] = theta
            div = bh[k, at, :] + diff[:, part]
            out.append(total[k] + bcc[k, at, :] * theta + damping * div)
        return out

    def early(n, slot):
        out = batch(n, SECOND, 4 * N)
        for k in HALVES:
            for s in range(4):
                gs[slot, s, k] = out[k][s * N : (s + 1) * N]
        for s in range(4):
            side(slot, s).start()

    def ring(n):
        out = batch(n, RING, 0)
        grid = grid_of(n + 1)
        for k in HALVES:
            for s in range(4):
                grid[k, line(RING[s]), :] = out[k][s * N : (s + 1) * N]

    def ring_state():
        for s in range(4):
            second(s).wait_recv()
        for c in range(4):
            corner(0, c).wait_recv()
        last = lax.broadcasted_iota(jnp.int32, (N, LANES), 0) == N - 1
        for k in HALVES:
            extra = (
                us[k, pl.ds(0, N), :], None, vflat[k, pl.ds(0, N, STRIDE), :], None,
            )
            end = (kr[0, 1, pl.ds(4 + k, 1), :], kr[0, 3, pl.ds(4 + k, 1), :],
                   kr[0, 2, pl.ds(2 + k, 1), :], kr[0, 3, pl.ds(2 + k, 1), :])
            for s in range(4):
                at = pl.ds(s * N, N)
                bth[k, at, :] = sr[s, 0, k]
                high, low = split(sr[s, 1, k])
                bxh[at, lanes(k)] = high
                bxl[at, lanes(k)] = low
                bcc[k, at, :] = sr[s, 2, k]
                h = sr[s, 3, k] + jnp.where(last, end[s], 0.0)
                bh0[k, at, :] = h if extra[s] is None else h + extra[s]
                ga[k, line(OUTER[s]), :] = sr[s, 4, k]
                x, y = CORNER_AT[s]
                ga[k, pl.ds(row(x, y), 1), :] = kr[0, s, pl.ds(k, 1), :]

    def receive(n, slot):
        grid = grid_of(n)
        for s in range(4):
            side(slot, s).wait_recv()
            corner(slot + 1, s).wait_recv()
        for k in HALVES:
            for s in range(4):
                grid[k, line(OUTER[s]), :] = gr[slot, s, k]
                x, y = CORNER_AT[s]
                grid[k, pl.ds(row(x, y), 1), :] = kr[slot + 1, s, pl.ds(k, 1), :]

    def prepare(n, b):
        grid = grid_of(n)
        at = pl.ds(b * BR, BR)
        for k in HALVES:
            laps = []
            for i in range(BX):
                lap, here = laplacian(grid, k, ("x", b * BX + i))
                laps.append(lap)
                if n == SUBSTEPS:
                    x = b * BX + i
                    west = grid[k, pl.ds(row(x - 1, 0), N), :]
                    south = grid[k, pl.ds(row(x, -1), N), :]
                    own = pl.ds(x * N, N)
                    u_o[own, lanes(k)] = us[k, own, :] + (here - west)
                    v_o[own, lanes(k)] = vs[k, x, pl.ds(0, N), :] + (here - south)
            h = h0[k, at, :] + jnp.concatenate(laps, axis=0)
            hh[k, at, :] = h
            high, low = split(th[k, at, :] - courant * h)
            xh[at, pl.ds(LV + k * LANES, LANES)] = high
            xl[at, pl.ds(LV + k * LANES, LANES)] = low

    def multiply(b):
        at = pl.ds(b * BR, BR)
        qs[b % 2] = product(xh[at, :], xl[at, :])

    def finish(n, b):
        at = pl.ds(b * BR, BR)
        upward = qs[b % 2, :, pl.ds(0, LV)]
        diff = vertical(upward)
        for k in HALVES:
            part = slice(k * LANES, (k + 1) * LANES)
            theta = qs[b % 2, :, pl.ds(LV + k * LANES, LANES)]
            div = hh[k, at, :] + diff[:, part]
            density = rho[k, at, :] - courant * div
            if n == SUBSTEPS:
                rho_o[at, lanes(k)] = density
                w_o[at, lanes(k)] = upward[:, part]
                th_o[at, lanes(k)] = theta
                continue
            rho[k, at, :] = density
            th[k, at, :] = theta
            high, low = split(upward[:, part])
            xh[at, lanes(k)] = high
            xl[at, lanes(k)] = low
            g = cc[k, at, :] * theta + damping * div
            for i in range(BX):
                own = pl.ds(row(b * BX + i, 0), N)
                grid_of(n + 1)[k, own, :] = grid_of(n)[k, own, :] + g[i * N : (i + 1) * N]

    def main(n):
        prepare(n, 0)
        for b in range(BLOCKS):
            if b + 1 < BLOCKS:
                prepare(n, b + 1)
            multiply(b)
            if b > 0:
                finish(n, b - 1)
        finish(n, BLOCKS - 1)

    def corners(n, slot):
        grid = grid_of(n)
        for c in range(4):
            x, y = CORNER_FROM[c]
            for k in HALVES:
                ks[slot, c, pl.ds(k, 1), :] = grid[k, pl.ds(row(x, y), 1), :]
        for c in range(4):
            corner(slot, c).start()

    early(1, 0)
    main(1)
    corners(2, 1)
    ring_state()
    ring(1)

    def pair(i, carry):
        for n in (2, 3):
            slot = 2 * i + n - 2
            early(n, slot + 1)
            main(n)
            corners(n + 1, slot + 2)
            receive(n, slot)
            ring(n)
        return carry

    lax.fori_loop(0, 2, pair, 0)
    main(SUBSTEPS)

    for s in range(4):
        side(4, s).wait_recv()
        corner(5, s).wait_recv()
        critical(s).wait_send()
        second(s).wait_send()
        corner(0, s).wait_send()
        for slot in range(5):
            side(slot, s).wait_send()
            corner(slot + 1, s).wait_send()


def body(density, flux_east, flux_north, flux_up, theta_pert, sound_coef, vert_inverse):
    flat = (ROWS, LV)
    half = pltpu.VMEM((2, ROWS, LANES), f32)
    plane = (2, N, LANES)
    any_space = pl.BlockSpec(memory_space=pl.ANY)
    vmem = pl.BlockSpec(memory_space=pltpu.VMEM)
    dma = pltpu.SemaphoreType.DMA
    outs = pl.pallas_call(
        kernel,
        out_shape=[jax.ShapeDtypeStruct(flat, f32)] * 5,
        in_specs=[any_space] * 7,
        out_specs=[vmem] * 5,
        scratch_shapes=[
            half,
            pltpu.VMEM((2, ROWS + N, LANES), f32),
            pltpu.VMEM((2, N, STRIDE, LANES), f32),
            half,
            half,
            pltpu.VMEM(flat, bf16),
            half,
            half,
            half,
            pltpu.VMEM((2 * LV, 2 * LV), f32),
            pltpu.VMEM((2 * LV, 2 * LV), bf16),
            pltpu.VMEM((2 * LV, 2 * LV), bf16),
            pltpu.VMEM((ROWS, 2 * LV), bf16),
            pltpu.VMEM((ROWS, 2 * LV), bf16),
            pltpu.VMEM((2, BR, 2 * LV), f32),
            pltpu.VMEM((2, PADDED, LANES), f32),
            pltpu.VMEM((2, PADDED, LANES), f32),
            pltpu.VMEM((2, 8 * N, LANES), f32),
            pltpu.VMEM((8 * N, 2 * LV), bf16),
            pltpu.VMEM((8 * N, 2 * LV), bf16),
            pltpu.VMEM((2, 8 * N, LANES), f32),
            pltpu.VMEM((2, 8 * N, LANES), f32),
            pltpu.VMEM((2, 8 * N, LANES), f32),
            pltpu.VMEM((4, 2) + plane, f32),
            pltpu.VMEM((4, 2) + plane, f32),
            pltpu.VMEM((4, 5) + plane, f32),
            pltpu.VMEM((4, 5) + plane, f32),
            pltpu.VMEM((5, 4) + plane, f32),
            pltpu.VMEM((5, 4) + plane, f32),
            pltpu.VMEM((6, 4, 8, LANES), f32),
            pltpu.VMEM((6, 4, 8, LANES), f32),
            dma((12,)),
            dma((4,)), dma((4,)),
            dma((4,)), dma((4,)),
            dma((5, 4)), dma((5, 4)),
            dma((6, 4)), dma((6, 4)),
        ],
        compiler_params=pltpu.CompilerParams(
            collective_id=0, has_side_effects=True, vmem_limit_bytes=50 * 1024 * 1024
        ),
    )(
        density.reshape(flat),
        flux_east.reshape(flat),
        flux_north,
        flux_up.reshape(flat),
        theta_pert.reshape(flat),
        sound_coef.reshape(flat),
        vert_inverse,
    )
    return tuple(out.reshape(N, N, LV) for out in outs)


def solution(mesh):
    block = P("gx", "gy", None)
    return jax.shard_map(
        body,
        mesh=mesh,
        in_specs=(block,) * 6 + (P(),),
        out_specs=(block,) * 5,
        check_vma=False,
    )
```

profile of v0, /device:TPU:1, one launch (start us, length us, event | category | flops | bytes accessed | tf_op | source)
XLA Modules:
  0.0 51.6 jit_solution(4510049484654332947)
XLA Ops:
  0.6 0.0 copy-start
  0.6 1.0 %copy-done = bf16[32,32,256]{2,1,0:T(8,128)(2,1)S(1)} copy-done((bf16[32,32,256]{2,1,0:T(8,128)(2,1)S(1)}, bf16[32,32,256]{2,1,0:T(8,128)(2,1)}, u32[]{:S(2)}) %copy-start) | copy-done | bytes 524312
  1.7 43.8 %shard_map.110 = (f32[1024,256]{1,0:T(8,128)S(1)}, f32[1024,256]{1,0:T(8,128)S(1)}, f32[1024,256]{1,0:T(8,128)S(1)}, f32[1024,256]{1,0:T(8,128)}, f32[1024,256]{1,0:T(8,128)}) custom-call(f32[1024,256]{1,0:T(8,128)} %bitcast.16, f32[1024,256]{1,0:T(8,128)} %bitcast.17, f32[32,32,256]{2,1,0:T(8,128)} %v_h.1, f32[1024,256]{1,0:T(8,128)} %bitcast.18, ...), custom_call_target="tpu_custom_call" | custom-call | tf_op jit(solution)/shard_map/pallas_call | solution.py:427
  45.5 1.0 %copy.17 = f32[32,32,256]{2,1,0:T(8,128)} copy(f32[32,32,256]{2,1,0:T(8,128)S(1)} %bitcast.12) | data formatting | bytes 2097152
  46.4 1.0 %copy.18 = f32[32,32,256]{2,1,0:T(8,128)} copy(f32[32,32,256]{2,1,0:T(8,128)S(1)} %bitcast.11) | data formatting | bytes 2097152
  47.4 0.0 copy-start.2
  47.4 1.0 %copy.19 = f32[32,32,256]{2,1,0:T(8,128)} copy(f32[32,32,256]{2,1,0:T(8,128)S(1)} %bitcast.10) | data formatting | bytes 2097152
  48.4 0.6 %copy-done.2 = f32[1024,256]{1,0:T(8,128)S(1)} copy-done((f32[1024,256]{1,0:T(8,128)S(1)}, f32[1024,256]{1,0:T(8,128)}, u32[]{:S(2)}) %copy-start.2) | copy-done | bytes 1048600
  49.0 0.0 copy-start.1
  49.0 1.0 %copy.20 = f32[32,32,256]{2,1,0:T(8,128)} copy(f32[32,32,256]{2,1,0:T(8,128)S(1)} %bitcast.15) | data formatting | bytes 2097152
  50.0 0.6 %copy-done.1 = f32[1024,256]{1,0:T(8,128)S(1)} copy-done((f32[1024,256]{1,0:T(8,128)S(1)}, f32[1024,256]{1,0:T(8,128)}, u32[]{:S(2)}) %copy-start.1) | copy-done | bytes 1048600
  50.6 1.0 %copy.21 = f32[32,32,256]{2,1,0:T(8,128)} copy(f32[32,32,256]{2,1,0:T(8,128)S(1)} %bitcast.14) | data formatting | bytes 2097152
Async XLA Ops:
  0.6 1.0 %copy-start = (bf16[32,32,256]{2,1,0:T(8,128)(2,1)S(1)}, bf16[32,32,256]{2,1,0:T(8,128)(2,1)}, u32[]{:S(2)}) copy-start(bf16[32,32,256]{2,1,0:T(8,128)(2,1)} %param.12) | copy-start | bytes 1572868
  47.4 1.6 %copy-start.2 = (f32[1024,256]{1,0:T(8,128)S(1)}, f32[1024,256]{1,0:T(8,128)}, u32[]{:S(2)}) copy-start(f32[1024,256]{1,0:T(8,128)} %get-tuple-element.13) | copy-start | bytes 3145732
  49.0 1.6 %copy-start.1 = (f32[1024,256]{1,0:T(8,128)S(1)}, f32[1024,256]{1,0:T(8,128)}, u32[]{:S(2)}) copy-start(f32[1024,256]{1,0:T(8,128)} %get-tuple-element.14) | copy-start | bytes 3145732
where the time goes:
time: 51.8 us; the launch traced here: 51.6 us
  Pallas kernels  43.8 us (85%)
  local copies, waits for them, and re-layouts  7.15 us (14%)
  between operations  0.65 us (1%)
    pallas_call x1, Pallas kernels, body(): pl.pallas_call(kernel, out_shape=[jax.ShapeDtypeStruct(flat, f32)] * 5, i...  43.8 us
    unnamed x11, local copies, waits for them, and re-layouts  7.15 us

commit v1 on v0

--- a/solution.py
+++ b/solution.py
@@ -22,6 +22,7 @@
 BX = 4
 BR = BX * N
 BLOCKS = N // BX
+CORNER_ROWS = 16
 RING = (("x", -1), ("x", N), ("y", -1), ("y", N))
 FIRST = (("x", N - 1), ("x", 0), ("y", N - 1), ("y", 0))
 SECOND = (("x", N - 2), ("x", 1), ("y", N - 2), ("y", 1))
@@ -57,10 +58,114 @@
     return high, (value - high.astype(f32)).astype(bf16)
 
 
+def vertical(upward):
+    first = lax.broadcasted_iota(jnp.int32, upward.shape, 1) == 0
+    return upward - jnp.where(first, 0.0, pltpu.roll(upward, 1, 1))
+
+
+def laplacian(grid, k, edge):
+    here = grid[k, line(edge), :]
+    around = (grid[k, line(edge, -1), :] + grid[k, line(edge, 1), :]) + (
+        grid[k, line(edge, 0, -1), :] + grid[k, line(edge, 0, 1), :]
+    )
+    return around - 4.0 * here, here
+
+
+def corner_laplacian(grid, k, x, y):
+    at = [grid[k, pl.ds(row(x + i, y + j), 1), :] for i, j in ((0, 0), (-1, 0), (1, 0), (0, -1), (0, 1))]
+    return (at[1] + at[2]) + (at[3] + at[4]) - 4.0 * at[0], at[0]
+
+
+def corner_rows(rows):
+    return jnp.concatenate(rows + [jnp.zeros((CORNER_ROWS - 4, LANES), f32)], axis=0)
+
+
+def product(mh, ml, parts):
+    total = None
+    for high, low, depth in parts:
+        for left, right in ((high, mh), (low, mh), (high, ml)):
+            term = jnp.dot(left, right[depth, :], preferred_element_type=f32)
+            total = term if total is None else total + term
+    return total
+
+
+def pipeline(grid, h0, th, hh, tth, ttl, wh, wl, mh, ml, qs, finish, extra=None):
+    def prepare(b):
+        at = pl.ds(b * BR, BR)
+        for k in HALVES:
+            laps = []
+            for i in range(BX):
+                lap, here = laplacian(grid, k, ("x", b * BX + i))
+                laps.append(lap)
+                if extra is not None:
+                    extra(k, b * BX + i, here)
+            h = h0[k, at, :] + jnp.concatenate(laps, axis=0)
+            hh[k, at, :] = h
+            high, low = split(th[k, at, :] - courant * h)
+            tth[at, lanes(k)] = high
+            ttl[at, lanes(k)] = low
+
+    def multiply(b):
+        at = pl.ds(b * BR, BR)
+        qs[b % 2] = product(mh, ml, [
+            (wh[at, :], wl[at, :], pl.ds(0, LV)),
+            (tth[at, :], ttl[at, :], pl.ds(LV, LV)),
+        ])
+
+    prepare(0)
+    for b in range(BLOCKS):
+        if b + 1 < BLOCKS:
+            prepare(b + 1)
+        multiply(b)
+        if b > 0:
+            finish(b - 1)
+    finish(BLOCKS - 1)
+
+
+def last_kernel(
+    rho, us, vs, th, h0, mh, ml, wh, wl, grid,
+    rho_h, u_h, v_h, w_h, th_h,
+    rho_o, u_o, v_o, w_o, th_o, hh, tth, ttl, qs, sem,
+):
+    copies = []
+
+    def store(src, dst, b):
+        at = pl.ds(b * BR, BR)
+        copy = pltpu.make_async_copy(src.at[at], dst.at[at], sem.at[len(copies)])
+        copy.start()
+        copies.append(copy)
+
+    def extra(k, x, here):
+        own = pl.ds(x * N, N)
+        west = grid[k, pl.ds(row(x - 1, 0), N), :]
+        south = grid[k, pl.ds(row(x, -1), N), :]
+        u_o[own, lanes(k)] = us[k, own, :] + (here - west)
+        v_o[own, lanes(k)] = vs[k, x, pl.ds(0, N), :] + (here - south)
+
+    def finish(b):
+        at = pl.ds(b * BR, BR)
+        upward = qs[b % 2, :, pl.ds(0, LV)]
+        diff = vertical(upward)
+        w_o[at, :] = upward
+        th_o[at, :] = qs[b % 2, :, pl.ds(LV, LV)]
+        for k in HALVES:
+            div = hh[k, at, :] + diff[:, k * LANES : (k + 1) * LANES]
+            rho_o[at, lanes(k)] = rho[k, at, :] - courant * div
+        store(u_o, u_h, b)
+        store(v_o, v_h, b)
+        store(rho_o, rho_h, b)
+        store(w_o, w_h, b)
+        store(th_o, th_h, b)
+
+    pipeline(grid, h0, th, hh, tth, ttl, wh, wl, mh, ml, qs, finish, extra)
+    for copy in copies:
+        copy.wait()
+
+
 def kernel(
     rho_h, u_h, v_h, w_h, th_h, cf_h, m_h,
-    rho_o, u_o, v_o, w_o, th_o,
-    rho, us, vs, ws, th, cf, cc, h0, hh, ms, mh, ml, xh, xl, qs, ga, gb,
+    rho, us, vs, th, h0, mh, ml, wh, wl, gb,
+    ws, cf, cc, hh, ms, tth, ttl, qs, ga,
     bth, bxh, bxl, bh0, bh, bcc,
     cs, cr, ss, sr, gs, gr, ks, kr,
     lsem, csem, crem, ssem, srem, gsem, grem, ksem, krem,
@@ -184,8 +289,8 @@
         at = pl.ds(pl.multiple_of(b * BR, BR), BR)
         for k in HALVES:
             high, low = split(ws[k, at, :])
-            xh[at, lanes(k)] = high
-            xl[at, lanes(k)] = low
+            wh[at, lanes(k)] = high
+            wl[at, lanes(k)] = low
         return carry
 
     lax.fori_loop(0, BLOCKS, first_w, 0)
@@ -195,6 +300,8 @@
             high, low = split(ms[pl.ds(i * 128, 128), pl.ds(j * 128, 128)].T)
             mh[pl.ds(j * 128, 128), pl.ds(i * 128, 128)] = high
             ml[pl.ds(j * 128, 128), pl.ds(i * 128, 128)] = low
+
+    own_corners = [pl.ds(x * N + y, 1) for x, y in CORNER_FROM]
 
     def early_state(s, k):
         at = pl.ds(N * 4 + s * N, N)
@@ -208,6 +315,12 @@
     for k in HALVES:
         for s in range(4):
             early_state(s, k)
+        at = pl.ds(8 * N, CORNER_ROWS)
+        bth[k, at, :] = corner_rows([th[k, own, :] for own in own_corners])
+        bcc[k, at, :] = corner_rows([cc[k, own, :] for own in own_corners])
+        high, low = split(corner_rows([ws[k, own, :] for own in own_corners]))
+        bxh[at, lanes(k)] = high
+        bxl[at, lanes(k)] = low
 
     for copy in load_rho:
         copy.wait()
@@ -223,38 +336,25 @@
         h0[k, last_y, :] = h0[k, last_y, :] + cr[3, 1, k]
         for s in range(4):
             bh0[k, pl.ds(N * 4 + s * N, N), :] = h0[k, compact(SECOND[s]), :]
-
-    first_lane = lax.broadcasted_iota(jnp.int32, (BR, LV), 1) == 0
-
-    def product(high, low):
-        q = jnp.dot(high, mh[...], preferred_element_type=f32)
-        q = q + jnp.dot(low, mh[...], preferred_element_type=f32)
-        return q + jnp.dot(high, ml[...], preferred_element_type=f32)
-
-    def vertical(upward):
-        below = jnp.where(first_lane, 0.0, pltpu.roll(upward, 1, 1))
-        return upward - below
-
-    def laplacian(grid, k, edge):
-        here = grid[k, line(edge), :]
-        around = (grid[k, line(edge, -1), :] + grid[k, line(edge, 1), :]) + (
-            grid[k, line(edge, 0, -1), :] + grid[k, line(edge, 0, 1), :]
-        )
-        return around - 4.0 * here, here
-
-    def batch(n, edges, base):
+        bh0[k, pl.ds(8 * N, CORNER_ROWS), :] = corner_rows([h0[k, own, :] for own in own_corners])
+
+    def batch(n, edges, base, with_corners):
         grid = grid_of(n)
-        at = pl.ds(base, 4 * N)
+        at = pl.ds(base, 4 * N + (CORNER_ROWS if with_corners else 0))
         total = []
         for k in HALVES:
             laps, heres = zip(*[laplacian(grid, k, edge) for edge in edges])
+            if with_corners:
+                more = [corner_laplacian(grid, k, x, y) for x, y in CORNER_FROM]
+                laps += (corner_rows([lap for lap, _ in more]),)
+                heres += (corner_rows([here for _, here in more]),)
             total.append(jnp.concatenate(heres, axis=0))
             h = bh0[k, at, :] + jnp.concatenate(laps, axis=0)
             bh[k, at, :] = h
             high, low = split(bth[k, at, :] - courant * h)
             bxh[at, pl.ds(LV + k * LANES, LANES)] = high
             bxl[at, pl.ds(LV + k * LANES, LANES)] = low
-        q = product(bxh[at, :], bxl[at, :])
+        q = product(mh, ml, [(bxh[at, :], bxl[at, :], pl.ds(0, 2 * LV))])
         diff = vertical(q[:, :LV])
         out = []
         for k in HALVES:
@@ -269,15 +369,17 @@
         return out
 
     def early(n, slot):
-        out = batch(n, SECOND, 4 * N)
+        out = batch(n, SECOND, 4 * N, True)
         for k in HALVES:
             for s in range(4):
                 gs[slot, s, k] = out[k][s * N : (s + 1) * N]
+                ks[slot + 1, s, pl.ds(k, 1), :] = out[k][4 * N + s : 4 * N + s + 1]
         for s in range(4):
             side(slot, s).start()
+            corner(slot + 1, s).start()
 
     def ring(n):
-        out = batch(n, RING, 0)
+        out = batch(n, RING, 0, False)
         grid = grid_of(n + 1)
         for k in HALVES:
             for s in range(4):
@@ -319,77 +421,31 @@
                 x, y = CORNER_AT[s]
                 grid[k, pl.ds(row(x, y), 1), :] = kr[slot + 1, s, pl.ds(k, 1), :]
 
-    def prepare(n, b):
-        grid = grid_of(n)
-        at = pl.ds(b * BR, BR)
-        for k in HALVES:
-            laps = []
-            for i in range(BX):
-                lap, here = laplacian(grid, k, ("x", b * BX + i))
-                laps.append(lap)
-                if n == SUBSTEPS:
-                    x = b * BX + i
-                    west = grid[k, pl.ds(row(x - 1, 0), N), :]
-                    south = grid[k, pl.ds(row(x, -1), N), :]
-                    own = pl.ds(x * N, N)
-                    u_o[own, lanes(k)] = us[k, own, :] + (here - west)
-                    v_o[own, lanes(k)] = vs[k, x, pl.ds(0, N), :] + (here - south)
-            h = h0[k, at, :] + jnp.concatenate(laps, axis=0)
-            hh[k, at, :] = h
-            high, low = split(th[k, at, :] - courant * h)
-            xh[at, pl.ds(LV + k * LANES, LANES)] = high
-            xl[at, pl.ds(LV + k * LANES, LANES)] = low
-
-    def multiply(b):
-        at = pl.ds(b * BR, BR)
-        qs[b % 2] = product(xh[at, :], xl[at, :])
-
-    def finish(n, b):
-        at = pl.ds(b * BR, BR)
-        upward = qs[b % 2, :, pl.ds(0, LV)]
-        diff = vertical(upward)
-        for k in HALVES:
-            part = slice(k * LANES, (k + 1) * LANES)
-            theta = qs[b % 2, :, pl.ds(LV + k * LANES, LANES)]
-            div = hh[k, at, :] + diff[:, part]
-            density = rho[k, at, :] - courant * div
-            if n == SUBSTEPS:
-                rho_o[at, lanes(k)] = density
-                w_o[at, lanes(k)] = upward[:, part]
-                th_o[at, lanes(k)] = theta
-                continue
-            rho[k, at, :] = density
-            th[k, at, :] = theta
-            high, low = split(upward[:, part])
-            xh[at, lanes(k)] = high
-            xl[at, lanes(k)] = low
-            g = cc[k, at, :] * theta + damping * div
-            for i in range(BX):
-                own = pl.ds(row(b * BX + i, 0), N)
-                grid_of(n + 1)[k, own, :] = grid_of(n)[k, own, :] + g[i * N : (i + 1) * N]
-
     def main(n):
-        prepare(n, 0)
-        for b in range(BLOCKS):
-            if b + 1 < BLOCKS:
-                prepare(n, b + 1)
-            multiply(b)
-            if b > 0:
-                finish(n, b - 1)
-        finish(n, BLOCKS - 1)
-
-    def corners(n, slot):
-        grid = grid_of(n)
-        for c in range(4):
-            x, y = CORNER_FROM[c]
+        grid, later = grid_of(n), grid_of(n + 1)
+
+        def finish(b):
+            at = pl.ds(b * BR, BR)
+            upward = qs[b % 2, :, pl.ds(0, LV)]
+            diff = vertical(upward)
             for k in HALVES:
-                ks[slot, c, pl.ds(k, 1), :] = grid[k, pl.ds(row(x, y), 1), :]
-        for c in range(4):
-            corner(slot, c).start()
+                part = slice(k * LANES, (k + 1) * LANES)
+                theta = qs[b % 2, :, pl.ds(LV + k * LANES, LANES)]
+                div = hh[k, at, :] + diff[:, part]
+                rho[k, at, :] = rho[k, at, :] - courant * div
+                th[k, at, :] = theta
+                high, low = split(upward[:, part])
+                wh[at, lanes(k)] = high
+                wl[at, lanes(k)] = low
+                g = cc[k, at, :] * theta + damping * div
+                for i in range(BX):
+                    own = pl.ds(row(b * BX + i, 0), N)
+                    later[k, own, :] = grid[k, own, :] + g[i * N : (i + 1) * N]
+
+        pipeline(grid, h0, th, hh, tth, ttl, wh, wl, mh, ml, qs, finish)
 
     early(1, 0)
     main(1)
-    corners(2, 1)
     ring_state()
     ring(1)
 
@@ -398,13 +454,11 @@
             slot = 2 * i + n - 2
             early(n, slot + 1)
             main(n)
-            corners(n + 1, slot + 2)
             receive(n, slot)
             ring(n)
         return carry
 
     lax.fori_loop(0, 2, pair, 0)
-    main(SUBSTEPS)
 
     for s in range(4):
         side(4, s).wait_recv()
@@ -419,40 +473,48 @@
 
 def body(density, flux_east, flux_north, flux_up, theta_pert, sound_coef, vert_inverse):
     flat = (ROWS, LV)
-    half = pltpu.VMEM((2, ROWS, LANES), f32)
+    half_shape = (2, ROWS, LANES)
+    half = pltpu.VMEM(half_shape, f32)
+    operand = pltpu.VMEM(flat, bf16)
     plane = (2, N, LANES)
-    any_space = pl.BlockSpec(memory_space=pl.ANY)
+    batch_half = pltpu.VMEM((2, 8 * N + CORNER_ROWS, LANES), f32)
+    batch_operand = pltpu.VMEM((8 * N + CORNER_ROWS, 2 * LV), bf16)
+    hbm = pl.BlockSpec(memory_space=pltpu.HBM)
     vmem = pl.BlockSpec(memory_space=pltpu.VMEM)
     dma = pltpu.SemaphoreType.DMA
-    outs = pl.pallas_call(
+    shape = jax.ShapeDtypeStruct
+    state = pl.pallas_call(
         kernel,
-        out_shape=[jax.ShapeDtypeStruct(flat, f32)] * 5,
-        in_specs=[any_space] * 7,
-        out_specs=[vmem] * 5,
+        out_shape=[
+            shape(half_shape, f32),
+            shape((2, ROWS + N, LANES), f32),
+            shape((2, N, STRIDE, LANES), f32),
+            shape(half_shape, f32),
+            shape(half_shape, f32),
+            shape((2 * LV, 2 * LV), bf16),
+            shape((2 * LV, 2 * LV), bf16),
+            shape(flat, bf16),
+            shape(flat, bf16),
+            shape((2, PADDED, LANES), f32),
+        ],
+        in_specs=[hbm] * 7,
+        out_specs=[vmem] * 10,
         scratch_shapes=[
             half,
-            pltpu.VMEM((2, ROWS + N, LANES), f32),
-            pltpu.VMEM((2, N, STRIDE, LANES), f32),
-            half,
-            half,
-            pltpu.VMEM(flat, bf16),
-            half,
+            operand,
             half,
             half,
             pltpu.VMEM((2 * LV, 2 * LV), f32),
-            pltpu.VMEM((2 * LV, 2 * LV), bf16),
-            pltpu.VMEM((2 * LV, 2 * LV), bf16),
-            pltpu.VMEM((ROWS, 2 * LV), bf16),
-            pltpu.VMEM((ROWS, 2 * LV), bf16),
+            operand,
+            operand,
             pltpu.VMEM((2, BR, 2 * LV), f32),
             pltpu.VMEM((2, PADDED, LANES), f32),
-            pltpu.VMEM((2, PADDED, LANES), f32),
-            pltpu.VMEM((2, 8 * N, LANES), f32),
-            pltpu.VMEM((8 * N, 2 * LV), bf16),
-            pltpu.VMEM((8 * N, 2 * LV), bf16),
-            pltpu.VMEM((2, 8 * N, LANES), f32),
-            pltpu.VMEM((2, 8 * N, LANES), f32),
-            pltpu.VMEM((2, 8 * N, LANES), f32),
+            batch_half,
+            batch_operand,
+            batch_operand,
+            batch_half,
+            batch_half,
+            batch_half,
             pltpu.VMEM((4, 2) + plane, f32),
             pltpu.VMEM((4, 2) + plane, f32),
             pltpu.VMEM((4, 5) + plane, f32),
@@ -468,9 +530,9 @@
             dma((6, 4)), dma((6, 4)),
         ],
         compiler_params=pltpu.CompilerParams(
-            collective_id=0, has_side_effects=True, vmem_limit_bytes=50 * 1024 * 1024
+            collective_id=0, has_side_effects=True, vmem_limit_bytes=28 * 1024 * 1024
         ),
-    )(
+    )(*[pltpu.with_memory_space_constraint(array, pltpu.HBM) for array in (
         density.reshape(flat),
         flux_east.reshape(flat),
         flux_north,
@@ -478,7 +540,20 @@
         theta_pert.reshape(flat),
         sound_coef.reshape(flat),
         vert_inverse,
-    )
+    )])
+    out = pltpu.VMEM(flat, f32)
+    outs = pl.pallas_call(
+        last_kernel,
+        out_shape=[shape(flat, f32)] * 5,
+        in_specs=[vmem] * 10,
+        out_specs=[hbm] * 5,
+        scratch_shapes=[
+            out, out, out, out, out, half, operand, operand,
+            pltpu.VMEM((2, BR, 2 * LV), f32),
+            dma((5 * BLOCKS,)),
+        ],
+        compiler_params=pltpu.CompilerParams(vmem_limit_bytes=28 * 1024 * 1024),
+    )(*state)
     return tuple(out.reshape(N, N, LV) for out in outs)
 
 

time: 51.8 us -> 42.7 us (0.82)
  local copies, waits for them, and re-layouts: 7.15 us -> 0 us
  Pallas kernels: 43.8 us -> 41.5 us
    unnamed x11 -> x0, local copies, waits for them, and re-layouts: 7.15 us -> none
    pallas_call x1 -> x2, Pallas kernels: 43.8 us -> 41.5 us  [the longest x1 38.3 us: body(): pl.pallas_call(kernel, out_shape=[shape(half_shape, f32), shape((2, ROWS...]
where the time goes in v1:
time: 42.7 us; the launch traced here: 42.1 us
  Pallas kernels  41.5 us (97%)
  between operations  0.64 us (1%)
    pallas_call x1, Pallas kernels, body(): pl.pallas_call(kernel, out_shape=[shape(half_shape, f32), shape((2, ROWS...  38.3 us
    pallas_call x1, Pallas kernels, body(): pl.pallas_call(last_kernel, out_shape=[shape(flat, f32)] * 5, in_specs=[v...  3.19 us

profile of v1, /device:TPU:1, one launch (start us, length us, event | category | flops | bytes accessed | tf_op | source)
XLA Modules:
  0.0 42.1 jit_solution(10236165452186878068)
XLA Ops:
  0.6 38.3 %shard_map.110 = (f32[2,1024,128]{2,1,0:T(8,128)S(1)}, f32[2,1056,128]{2,1,0:T(8,128)S(1)}, f32[2,32,40,128]{3,2,1,0:T(8,128)S(1)}, f32[2,1024,128]{2,1,0:T(8,12...) custom-call(f32[1024,256]{1,0:T(8,128)} %bitcast.10, ...), custom_call_target="tpu_custom_call" | custom-call | tf_op jit(solution)/shard_map/pallas_call | solution.py:486
  38.9 3.2 %shard_map.111 = (f32[1024,256]{1,0:T(8,128)}, f32[1024,256]{1,0:T(8,128)}, f32[1024,256]{1,0:T(8,128)}, f32[1024,256]{1,0:T(8,128)}, f32[1024,256]{1,0:T(8,128)}) custom-call(f32[2,1024,128]{2,1,0:T(8,128)S(1)} %get-tuple-element.20.rho, f32[2,1056,128]{2,1,0:T(8,128)S(1)} %get-tuple-element.21.us, f32[2,32,40,128]{3,2,1,0:T(8,128)S(1)} %get-tuple-element.22.vs, ...), custom_call_target="tpu_custom_call" | custom-call | tf_op jit(solution)/shard_map/pallas_call | solution.py:545

commit v2 on v1

--- a/solution.py
+++ b/solution.py
@@ -23,6 +23,7 @@
 BR = BX * N
 BLOCKS = N // BX
 CORNER_ROWS = 16
+MESSAGES = SUBSTEPS - 2
 RING = (("x", -1), ("x", N), ("y", -1), ("y", N))
 FIRST = (("x", N - 1), ("x", 0), ("y", N - 1), ("y", 0))
 SECOND = (("x", N - 2), ("x", 1), ("y", N - 2), ("y", 1))
@@ -166,7 +167,7 @@
     rho_h, u_h, v_h, w_h, th_h, cf_h, m_h,
     rho, us, vs, th, h0, mh, ml, wh, wl, gb,
     ws, cf, cc, hh, ms, tth, ttl, qs, ga,
-    bth, bxh, bxl, bh0, bh, bcc,
+    bth, bxh, bxl, bh0, bh, bcc, bg1,
     cs, cr, ss, sr, gs, gr, ks, kr,
     lsem, csem, crem, ssem, srem, gsem, grem, ksem, krem,
 ):
@@ -191,9 +192,6 @@
     load_cf = load(cf_h, cf)
     load_u = [load(u_h.at[:, lanes(k)], us.at[k, pl.ds(0, ROWS)]) for k in HALVES]
     load_v = [load(v_h.at[:, :, lanes(k)], vs.at[k, :, pl.ds(0, N)]) for k in HALVES]
-    load_w = [load(w_h.at[:, lanes(k)], ws.at[k]) for k in HALVES]
-    load_m = load(m_h, ms)
-    load_rho = [load(rho_h.at[:, lanes(k)], rho.at[k]) for k in HALVES]
 
     barrier = pltpu.get_barrier_semaphore()
     for to in side_to + corner_to:
@@ -211,6 +209,9 @@
     for copy in load_th:
         copy.wait()
     load_cf.wait()
+    load_w = [load(w_h.at[:, lanes(k)], ws.at[k]) for k in HALVES]
+    load_m = load(m_h, ms)
+    load_rho = [load(rho_h.at[:, lanes(k)], rho.at[k]) for k in HALVES]
 
     def first_g(b, carry):
         at = pl.ds(pl.multiple_of(b * BR, BR), BR)
@@ -277,11 +278,11 @@
     for k in HALVES:
         for s in range(4):
             edge = compact(FIRST[s])
-            ss[s, 0, k] = th[k, edge, :]
-            ss[s, 1, k] = ws[k, edge, :]
-            ss[s, 2, k] = cc[k, edge, :]
-            ss[s, 3, k] = h0[k, edge, :]
-            ss[s, 4, k] = ga[k, line(SECOND[s]), :]
+            inner = ga[k, line(SECOND[s]), :]
+            bg1[k, pl.ds(s * N, N), :] = inner
+            ss[s, 0, k] = ws[k, edge, :]
+            ss[s, 1, k] = cc[k, edge, :]
+            ss[s, 2, k] = h0[k, edge, :] + inner
     for s in range(4):
         second(s).start()
 
@@ -372,7 +373,8 @@
         out = batch(n, SECOND, 4 * N, True)
         for k in HALVES:
             for s in range(4):
-                gs[slot, s, k] = out[k][s * N : (s + 1) * N]
+                part = slice(s * N, (s + 1) * N)
+                gs[slot, s, k] = out[k][part] - bg1[k, pl.ds(s * N, N), :]
                 ks[slot + 1, s, pl.ds(k, 1), :] = out[k][4 * N + s : 4 * N + s + 1]
         for s in range(4):
             side(slot, s).start()
@@ -399,14 +401,15 @@
                    kr[0, 2, pl.ds(2 + k, 1), :], kr[0, 3, pl.ds(2 + k, 1), :])
             for s in range(4):
                 at = pl.ds(s * N, N)
-                bth[k, at, :] = sr[s, 0, k]
-                high, low = split(sr[s, 1, k])
+                coef = sr[s, 1, k]
+                bth[k, at, :] = cr[s, 0, k] / coef
+                high, low = split(sr[s, 0, k])
                 bxh[at, lanes(k)] = high
                 bxl[at, lanes(k)] = low
-                bcc[k, at, :] = sr[s, 2, k]
-                h = sr[s, 3, k] + jnp.where(last, end[s], 0.0)
+                bcc[k, at, :] = coef
+                h = sr[s, 2, k] + jnp.where(last, end[s], 0.0)
                 bh0[k, at, :] = h if extra[s] is None else h + extra[s]
-                ga[k, line(OUTER[s]), :] = sr[s, 4, k]
+                ga[k, line(OUTER[s]), :] = jnp.zeros((N, LANES), f32)
                 x, y = CORNER_AT[s]
                 ga[k, pl.ds(row(x, y), 1), :] = kr[0, s, pl.ds(k, 1), :]
 
@@ -449,24 +452,18 @@
     ring_state()
     ring(1)
 
-    def pair(i, carry):
-        for n in (2, 3):
-            slot = 2 * i + n - 2
-            early(n, slot + 1)
-            main(n)
-            receive(n, slot)
-            ring(n)
-        return carry
-
-    lax.fori_loop(0, 2, pair, 0)
+    for n in range(2, SUBSTEPS):
+        if n < SUBSTEPS - 1:
+            early(n, n - 1)
+        main(n)
+        receive(n, n - 2)
+        ring(n)
 
     for s in range(4):
-        side(4, s).wait_recv()
-        corner(5, s).wait_recv()
         critical(s).wait_send()
         second(s).wait_send()
         corner(0, s).wait_send()
-        for slot in range(5):
+        for slot in range(MESSAGES):
             side(slot, s).wait_send()
             corner(slot + 1, s).wait_send()
 
@@ -515,19 +512,20 @@
             batch_half,
             batch_half,
             batch_half,
+            pltpu.VMEM((2, 4 * N, LANES), f32),
             pltpu.VMEM((4, 2) + plane, f32),
             pltpu.VMEM((4, 2) + plane, f32),
-            pltpu.VMEM((4, 5) + plane, f32),
-            pltpu.VMEM((4, 5) + plane, f32),
-            pltpu.VMEM((5, 4) + plane, f32),
-            pltpu.VMEM((5, 4) + plane, f32),
-            pltpu.VMEM((6, 4, 8, LANES), f32),
-            pltpu.VMEM((6, 4, 8, LANES), f32),
+            pltpu.VMEM((4, 3) + plane, f32),
+            pltpu.VMEM((4, 3) + plane, f32),
+            pltpu.VMEM((MESSAGES, 4) + plane, f32),
+            pltpu.VMEM((MESSAGES, 4) + plane, f32),
+            pltpu.VMEM((MESSAGES + 1, 4, 8, LANES), f32),
+            pltpu.VMEM((MESSAGES + 1, 4, 8, LANES), f32),
             dma((12,)),
             dma((4,)), dma((4,)),
             dma((4,)), dma((4,)),
-            dma((5, 4)), dma((5, 4)),
-            dma((6, 4)), dma((6, 4)),
+            dma((MESSAGES, 4)), dma((MESSAGES, 4)),
+            dma((MESSAGES + 1, 4)), dma((MESSAGES + 1, 4)),
         ],
         compiler_params=pltpu.CompilerParams(
             collective_id=0, has_side_effects=True, vmem_limit_bytes=28 * 1024 * 1024

time: 42.7 us -> 36.4 us (0.85); the launches traced: 42.1 us -> 36.3 us
  Pallas kernels: 41.5 us -> 35.5 us
    pallas_call x1, Pallas kernels: 38.3 us -> 32.3 us  [body(): pl.pallas_call(kernel, out_shape=[shape(half_shape, f32), shape((2, ROWS...]
where the time goes in v2:
time: 36.4 us; the launch traced here: 36.3 us
  Pallas kernels  35.5 us (98%)
  between operations  0.8 us (2%)
    pallas_call x1, Pallas kernels, body(): pl.pallas_call(kernel, out_shape=[shape(half_shape, f32), shape((2, ROWS...  32.3 us
    pallas_call x1, Pallas kernels, body(): pl.pallas_call(last_kernel, out_shape=[shape(flat, f32)] * 5, in_specs=[v...  3.19 us

profile of v2, /device:TPU:1, one launch (start us, length us, event | category | flops | bytes accessed | tf_op | source)
XLA Modules:
  0.0 36.3 jit_solution(3846432386202935769)
XLA Ops:
  0.6 32.3 %shard_map.110 = (f32[2,1024,128]{2,1,0:T(8,128)S(1)}, f32[2,1056,128]{2,1,0:T(8,128)S(1)}, f32[2,32,40,128]{3,2,1,0:T(8,128)S(1)}, f32[2,1024,128]{2,1,0:T(8,12...) custom-call(f32[1024,256]{1,0:T(8,128)} %bitcast.10, ...), custom_call_target="tpu_custom_call" | custom-call | tf_op jit(solution)/shard_map/pallas_call | solution.py:483
  33.0 3.2 %shard_map.111 = (f32[1024,256]{1,0:T(8,128)}, f32[1024,256]{1,0:T(8,128)}, f32[1024,256]{1,0:T(8,128)}, f32[1024,256]{1,0:T(8,128)}, f32[1024,256]{1,0:T(8,128)}) custom-call(f32[2,1024,128]{2,1,0:T(8,128)S(1)} %get-tuple-element.20.rho, f32[2,1056,128]{2,1,0:T(8,128)S(1)} %get-tuple-element.21.us, f32[2,32,40,128]{3,2,1,0:T(8,128)S(1)} %get-tuple-element.22.vs, ...), custom_call_target="tpu_custom_call" | custom-call | tf_op jit(solution)/shard_map/pallas_call | solution.py:543

commit v3 on v2

--- a/solution.py
+++ b/solution.py
@@ -19,7 +19,7 @@
 ROWS = N * N
 STRIDE = 40
 PADDED = (N + 4) * STRIDE + 8
-BX = 4
+BX = 8
 BR = BX * N
 BLOCKS = N // BX
 CORNER_ROWS = 16
@@ -192,6 +192,7 @@
     load_cf = load(cf_h, cf)
     load_u = [load(u_h.at[:, lanes(k)], us.at[k, pl.ds(0, ROWS)]) for k in HALVES]
     load_v = [load(v_h.at[:, :, lanes(k)], vs.at[k, :, pl.ds(0, N)]) for k in HALVES]
+    load_w = [load(w_h.at[:, lanes(k)], ws.at[k]) for k in HALVES]
 
     barrier = pltpu.get_barrier_semaphore()
     for to in side_to + corner_to:
@@ -209,7 +210,6 @@
     for copy in load_th:
         copy.wait()
     load_cf.wait()
-    load_w = [load(w_h.at[:, lanes(k)], ws.at[k]) for k in HALVES]
     load_m = load(m_h, ms)
     load_rho = [load(rho_h.at[:, lanes(k)], rho.at[k]) for k in HALVES]
 
@@ -263,6 +263,26 @@
     for c in range(4):
         corner(0, c).start()
 
+    for copy in load_w:
+        copy.wait()
+    for k in HALVES:
+        for s in range(4):
+            axis, at = FIRST[s]
+            edge = compact(FIRST[s])
+            if axis == "x":
+                beyond = pl.ds((at + 1) * N, N)
+                here, after = vs[k, at, pl.ds(0, N), :], vs[k, at, pl.ds(1, N), :]
+            else:
+                beyond = pl.ds(N + at, N, N)
+                here, after = vflat[k, pl.ds(at, N, STRIDE), :], vflat[k, pl.ds(at + 1, N, STRIDE), :]
+            inner = ga[k, line(SECOND[s]), :]
+            bg1[k, pl.ds(s * N, N), :] = inner
+            ss[s, 0, k] = ws[k, edge, :]
+            ss[s, 1, k] = cc[k, edge, :]
+            ss[s, 2, k] = (us[k, beyond, :] - us[k, edge, :]) + (after - here) + inner
+    for s in range(4):
+        second(s).start()
+
     def first_h(x, carry):
         at = pl.ds(pl.multiple_of(x * N, N), N)
         nxt = pl.ds(pl.multiple_of(x * N + N, N), N)
@@ -273,18 +293,6 @@
         return carry
 
     lax.fori_loop(0, N, first_h, 0)
-    for copy in load_w:
-        copy.wait()
-    for k in HALVES:
-        for s in range(4):
-            edge = compact(FIRST[s])
-            inner = ga[k, line(SECOND[s]), :]
-            bg1[k, pl.ds(s * N, N), :] = inner
-            ss[s, 0, k] = ws[k, edge, :]
-            ss[s, 1, k] = cc[k, edge, :]
-            ss[s, 2, k] = h0[k, edge, :] + inner
-    for s in range(4):
-        second(s).start()
 
     def first_w(b, carry):
         at = pl.ds(pl.multiple_of(b * BR, BR), BR)
@@ -376,9 +384,10 @@
                 part = slice(s * N, (s + 1) * N)
                 gs[slot, s, k] = out[k][part] - bg1[k, pl.ds(s * N, N), :]
                 ks[slot + 1, s, pl.ds(k, 1), :] = out[k][4 * N + s : 4 * N + s + 1]
+        for c in range(4):
+            corner(slot + 1, c).start()
         for s in range(4):
             side(slot, s).start()
-            corner(slot + 1, s).start()
 
     def ring(n):
         out = batch(n, RING, 0, False)

time: 36.4 us -> 36.7 us (level); the launches traced: 36.3 us -> 36 us
    pallas_call x1, Pallas kernels: 32.3 us -> 31.7 us  [body(): pl.pallas_call(kernel, out_shape=[shape(half_shape, f32), shape((2, ROWS...]
where the time goes in v3:
time: 36.7 us; the launch traced here: 36 us
  Pallas kernels  35.2 us (96%)
  between operations  0.8 us (2%)
    pallas_call x1, Pallas kernels, body(): pl.pallas_call(kernel, out_shape=[shape(half_shape, f32), shape((2, ROWS...  31.7 us
    pallas_call x1, Pallas kernels, body(): pl.pallas_call(last_kernel, out_shape=[shape(flat, f32)] * 5, in_specs=[v...  3.49 us

profile of v3, /device:TPU:1, one launch (start us, length us, event | category | flops | bytes accessed | tf_op | source)
XLA Modules:
  0.0 36.0 jit_solution(9323862664817560103)
XLA Ops:
  0.6 31.7 %shard_map.110 = (f32[2,1024,128]{2,1,0:T(8,128)S(1)}, f32[2,1056,128]{2,1,0:T(8,128)S(1)}, f32[2,32,40,128]{3,2,1,0:T(8,128)S(1)}, f32[2,1024,128]{2,1,0:T(8,12...) custom-call(f32[1024,256]{1,0:T(8,128)} %bitcast.10, ...), custom_call_target="tpu_custom_call" | custom-call | tf_op jit(solution)/shard_map/pallas_call | solution.py:492
  32.4 3.5 %shard_map.111 = (f32[1024,256]{1,0:T(8,128)}, f32[1024,256]{1,0:T(8,128)}, f32[1024,256]{1,0:T(8,128)}, f32[1024,256]{1,0:T(8,128)}, f32[1024,256]{1,0:T(8,128)}) custom-call(f32[2,1024,128]{2,1,0:T(8,128)S(1)} %get-tuple-element.20.rho, f32[2,1056,128]{2,1,0:T(8,128)S(1)} %get-tuple-element.21.us, f32[2,32,40,128]{3,2,1,0:T(8,128)S(1)} %get-tuple-element.22.vs, ...), custom_call_target="tpu_custom_call" | custom-call | tf_op jit(solution)/shard_map/pallas_call | solution.py:552

commit v4 on v3

--- a/solution.py
+++ b/solution.py
@@ -90,7 +90,7 @@
     return total
 
 
-def pipeline(grid, h0, th, hh, tth, ttl, wh, wl, mh, ml, qs, finish, extra=None):
+def pipeline(grid, h0, th, hh, tth, ttl, wh, wl, mh, ml, qs, finish, extra=None, ready=None):
     def prepare(b):
         at = pl.ds(b * BR, BR)
         for k in HALVES:
@@ -118,6 +118,8 @@
         if b + 1 < BLOCKS:
             prepare(b + 1)
         multiply(b)
+        if ready is not None:
+            ready(b)
         if b > 0:
             finish(b - 1)
     finish(BLOCKS - 1)
@@ -152,13 +154,15 @@
         for k in HALVES:
             div = hh[k, at, :] + diff[:, k * LANES : (k + 1) * LANES]
             rho_o[at, lanes(k)] = rho[k, at, :] - courant * div
-        store(u_o, u_h, b)
-        store(v_o, v_h, b)
         store(rho_o, rho_h, b)
         store(w_o, w_h, b)
         store(th_o, th_h, b)
 
-    pipeline(grid, h0, th, hh, tth, ttl, wh, wl, mh, ml, qs, finish, extra)
+    def ready(b):
+        store(u_o, u_h, b)
+        store(v_o, v_h, b)
+
+    pipeline(grid, h0, th, hh, tth, ttl, wh, wl, mh, ml, qs, finish, extra, ready)
     for copy in copies:
         copy.wait()
 

time: 36.7 us -> 36.5 us (level)
  no operation moved by 1% of the time
where the time goes in v4:
time: 36.5 us; the launch traced here: 35.8 us
  Pallas kernels  35 us (96%)
  between operations  0.8 us (2%)
    pallas_call x1, Pallas kernels, body(): pl.pallas_call(kernel, out_shape=[shape(half_shape, f32), shape((2, ROWS...  31.7 us
    pallas_call x1, Pallas kernels, body(): pl.pallas_call(last_kernel, out_shape=[shape(flat, f32)] * 5, in_specs=[v...  3.3 us

profile of v4, /device:TPU:1, one launch (start us, length us, event | category | flops | bytes accessed | tf_op | source)
XLA Modules:
  0.0 35.8 jit_solution(7660279863392098165)
XLA Ops:
  0.6 31.7 %shard_map.110 = (f32[2,1024,128]{2,1,0:T(8,128)S(1)}, f32[2,1056,128]{2,1,0:T(8,128)S(1)}, f32[2,32,40,128]{3,2,1,0:T(8,128)S(1)}, f32[2,1024,128]{2,1,0:T(8,12...) custom-call(f32[1024,256]{1,0:T(8,128)} %bitcast.10, ...), custom_call_target="tpu_custom_call" | custom-call | tf_op jit(solution)/shard_map/pallas_call | solution.py:496
  32.4 3.3 %shard_map.111 = (f32[1024,256]{1,0:T(8,128)}, f32[1024,256]{1,0:T(8,128)}, f32[1024,256]{1,0:T(8,128)}, f32[1024,256]{1,0:T(8,128)}, f32[1024,256]{1,0:T(8,128)}) custom-call(f32[2,1024,128]{2,1,0:T(8,128)S(1)} %get-tuple-element.20.rho, f32[2,1056,128]{2,1,0:T(8,128)S(1)} %get-tuple-element.21.us, f32[2,32,40,128]{3,2,1,0:T(8,128)S(1)} %get-tuple-element.22.vs, ...), custom_call_target="tpu_custom_call" | custom-call | tf_op jit(solution)/shard_map/pallas_call | solution.py:556
